TPU v7x, 32 devices: a whole 2x2x4 slice. The times are simulated.
32 devices in a mesh: dp: 8 (over y, x, core), mp: 4 (over z).
Axes of the slice: x: 2, y: 2, z: 4, core: 2. Of those that a mesh axis runs over, the one named last changes fastest.
Arguments:
- train_acts: bfloat16 [4096, 2560], P('dp'), may hold values from -6 to 6
- train_grads: bfloat16 [4096, 2560], P('dp'), may hold values from -6 to 6
- lengths: int32 [32], P('dp'), may hold values from 1 to 256, as said below
- query_acts: bfloat16 [128, 2560], replicated, may hold values from -6 to 6
- query_grads: bfloat16 [128, 2560], replicated, may hold values from -0.0059814453 to 0.0059814453
- basis_in: bfloat16 [2560, 2560], P(None, 'mp'), may hold values from -0.125 to 0.125
- basis_out: bfloat16 [2560, 2560], P(None, 'mp'), may hold values from -0.125 to 0.125
Outputs:
- scores: float32 [1, 32], P(None, 'dp')
Inputs may be any that keep to these rules, and one draw needn't show every extreme that they name: The 4 lengths of one index of dp sum to at most 512; in every draw some index's sequences fill all 512 rows and one of them has exactly 256 tokens.
All inputs are finite; a program needn't handle non-finite values.
Results may differ from a plain program's by a relative error of at most 0.0045.
Values may be sent and summed in bfloat16 or wider, within the bound.
A program may use at most 128 MiB of HBM per device.

v0:
```python
import jax
import jax.numpy as jnp
from jax import lax
from jax.sharding import PartitionSpec as P

QUERIES = 1
QLEN = 128
damping_ratio = 0.1


def rotate(values, basis):
    return jnp.dot(values, basis, preferred_element_type=jnp.float32).astype(jnp.bfloat16)


def shards(train_acts, train_grads, lengths, query_acts, query_grads, basis_in, basis_out):
    capacity = train_acts.shape[0]
    window = capacity // 2
    slot_count = lengths.shape[0]
    acts_block = rotate(train_acts, basis_in)
    query_block = rotate(query_acts, basis_in)
    acts_rot, query_rot = (
        lax.all_gather(acts_block, "mp", axis=1, tiled=True),
        lax.all_gather(query_block, "mp", axis=1, tiled=True),
    )
    grads_rot = rotate(train_grads, basis_out)
    query_grot = rotate(query_grads, basis_out).reshape(QUERIES, QLEN, -1)
    finish = jnp.cumsum(lengths)
    starts = finish - lengths
    position = jnp.arange(window, dtype=jnp.int32)
    curvature_local = jnp.zeros((grads_rot.shape[1], acts_rot.shape[1]), jnp.float32)
    stored_list = []
    for slot in range(slot_count):
        begin = jnp.minimum(starts[slot], capacity - window)
        grads_win = lax.dynamic_slice_in_dim(grads_rot, begin, window, 0)
        acts_win = lax.dynamic_slice_in_dim(acts_rot, begin, window, 0)
        inside = (position + begin >= starts[slot]) & (position + begin < finish[slot])
        grads_win = jnp.where(inside[:, None], grads_win, jnp.zeros_like(grads_win))
        product = lax.dot_general(
            grads_win, acts_win, (((0,), (0,)), ((), ())), preferred_element_type=jnp.float32
        )
        curvature_local = curvature_local + product * product
        stored_list.append(product.astype(jnp.bfloat16))
    stored = jnp.stack(stored_list)
    inverse_count = 1.0 / (slot_count * lax.axis_size("dp"))
    query_full = query_rot.reshape(QUERIES, QLEN, -1)
    curvature = lax.psum(curvature_local, "dp") * inverse_count
    grand_total = lax.psum(jnp.sum(curvature), "mp")
    damping = damping_ratio * grand_total / (curvature.size * lax.axis_size("mp"))
    local_grad = jnp.einsum(
        "qti,qtj->qij", query_grot, query_full, preferred_element_type=jnp.float32
    )
    precond = (local_grad / (curvature + damping)).astype(jnp.bfloat16)
    partial_value = jnp.einsum("qik,sik->qs", precond, stored, preferred_element_type=jnp.float32)
    return lax.psum(partial_value, "mp")


def solution(mesh):
    return jax.shard_map(
        shards,
        mesh=mesh,
        in_specs=(P("dp", None), P("dp", None), P("dp"), P(), P(), P(None, "mp"), P(None, "mp")),
        out_specs=P(None, "dp"),
        check_vma=False,
    )
```

profile of v0, /device:TPU:0, one launch (start us, length us, event | category | flops | bytes accessed | tf_op | source)
XLA Modules:
  0.0 276.5 jit_solution(13242700860598171906)
XLA Ops:
  6.5 0.0 copy-start
  6.5 0.0 copy-start.5
  6.5 0.0 all-gather.2.cloned.1.call-start
  6.5 5.9 %convolution_convert_fusion = bf16[512,640]{1,0:T(8,128)(2,1)} fusion(bf16[512,2560]{1,0:T(8,128)(2,1)} %param.7, bf16[2560,640]{1,0:T(8,128)(2,1)} %param.12), kind=kOutput, calls=%fused_computation.12 | convolution fusion | flops 1678049280 | bytes 6553600 | tf_op jit(solution)/shard_map/dot_general | solution.py:12
  12.4 0.0 all-gather.2.cloned.1.call-update
  12.5 0.0 all-reduce.2.cloned.1.call-start
  12.5 0.0 copy-done.5
  12.5 0.2 reduce-window.4
  12.7 0.6 fusion.42
  15.9 0.6 fusion.41
  16.5 1.2 compare_and_fusion.1
  17.7 1.3 compare_and_fusion.2
  19.0 1.3 compare_and_fusion
  20.2 1.3 compare_and_fusion.3
  21.5 0.0 copy-done
  21.5 5.0 %convolution_convert_fusion.1 = bf16[512,640]{1,0:T(8,128)(2,1)} fusion(bf16[512,2560]{1,0:T(8,128)(2,1)} %param.8, bf16[2560,640]{1,0:T(8,128)(2,1)S(1)} %copy-done), kind=kOutput, calls=%fused_computation.13 | convolution fusion | flops 1678049280 | bytes 6553600 | tf_op jit(solution)/shard_map/dot_general | solution.py:12
  26.5 43.4 %all-gather.2.cloned.1.call-done = bf16[512,2560]{1,0:T(8,128)(2,1)} async-done(((bf16[512,640]{1,0:T(8,128)(2,1)}), bf16[512,2560]{1,0:T(8,128)(2,1)}) %all-gather.2.cloned.1.call-update) | async-done | bytes 2621456 | tf_op jit(solution)/shard_map/all_gather | solution.py:22
  69.9 0.0 copy-start.3
  69.9 0.0 copy-start.4
  69.9 2.7 fusion.6
  72.7 0.0 copy-done.3
  72.7 0.0 copy-done.4
  72.7 3.9 %fusion.8 = f32[640,2560]{1,0:T(8,128)} fusion(bf16[512,2560]{1,0:T(8,128)(2,1)S(1)} %copy-done.3, s32[]{:T(128)S(6)} %select_n.31, bf16[512,640]{1,0:T(8,128)(2,1)S(1)} %copy-done.4, pred[256]{0:T(512)(128)(4,1)S(1)} %compare_and_fusion.2), kind=kOutput, calls=%fused_computation.18 | convolution fusion | flops 839024640 | bytes 8193536 | tf_op jit(solution)/shard_map/dot_general | solution.py:38
  76.6 3.9 %fusion.4 = f32[640,2560]{1,0:T(8,128)} fusion(bf16[512,2560]{1,0:T(8,128)(2,1)S(1)} %copy-done.3, s32[]{:T(128)S(6)} %select_n.35, bf16[512,640]{1,0:T(8,128)(2,1)S(1)} %copy-done.4, pred[256]{0:T(512)(128)(4,1)S(1)} %compare_and_fusion), kind=kOutput, calls=%fused_computation.14 | convolution fusion | flops 839024640 | bytes 8193536 | tf_op jit(solution)/shard_map/dot_general | solution.py:38
  80.5 17.1 %multiply_add_fusion = (f32[640,2560]{1,0:T(8,128)}, bf16[1,640,2560]{2,1,0:T(8,128)(2,1)}, bf16[1,640,2560]{2,1,0:T(8,128)(2,1)}, bf16[1,640,2560]{2,1,0:T(8,128)(2,1)}, bf16[1,640,2560]{2,1,0:T(8,128)(2,1)}) fusion(f32[640,2560]{1,0:T(8,128)} %fusion.4, f32[640,2560]{1,0:T(8,128)S(1)} %fusion.6, f32[640,2560]{1,0:T(8,128)} %fusion.8, ...), kind=kOutput, calls=%fused_computation.4 | convolution fusion | flops 857047040 | bytes 40961536 | tf_op jit(solution)/shard_map/dot_general | solution.py:38
  97.6 0.0 all-reduce.2.cloned.1.call-update
  97.6 2.8 %convolution_convert_fusion.2 = bf16[128,640]{1,0:T(8,128)(2,1)S(1)} fusion(bf16[128,2560]{1,0:T(8,128)(2,1)} %param.10, bf16[2560,640]{1,0:T(8,128)(2,1)} %param.12), kind=kOutput, calls=%fused_computation.22 | convolution fusion | flops 419512320 | bytes 4096000 | tf_op jit(solution)/shard_map/dot_general | solution.py:12
  100.5 17.4 %all_gather.6 = bf16[128,2560]{1,0:T(8,128)(2,1)} all-gather(bf16[128,640]{1,0:T(8,128)(2,1)S(1)} %convolution_convert_fusion.2), channel_id=1, replica_groups=mesh['dp'=8,'mp'=4] {'mp'}, dimensions={1}, use_global_device_ids=true | all-gather | bytes 819200 | tf_op jit(solution)/shard_map/all_gather | solution.py:23
  117.9 85.4 %all-reduce.2.cloned.1.call-done = f32[640,2560]{1,0:T(8,128)} async-done(((f32[640,2560]{1,0:T(8,128)}), f32[640,2560]{1,0:T(8,128)}) %all-reduce.2.cloned.1.call-update) | async-done | bytes 6553616 | tf_op jit(solution)/shard_map/psum | solution.py:46
  203.3 0.0 copy-start.1
  203.3 0.0 copy-start.2
  203.3 5.3 %multiply_reduce_fusion = f32[]{:T(128)} fusion(f32[640,2560]{1,0:T(8,128)} %all-reduce.2.cloned.1.call-done), kind=kLoop, calls=%fused_computation.6 | loop fusion | flops 3276799 | bytes 6553604 | tf_op jit(solution)/shard_map/reduce_sum | solution.py:47
  208.6 0.0 copy-done.1
  208.6 0.0 copy-done.2
  208.6 8.7 %pad_maximum_fusion = bf16[4,640,2560]{2,1,0:T(8,128)(2,1)} fusion(bf16[1,640,2560]{2,1,0:T(8,128)(2,1)} %get-tuple-element.9, bf16[1,640,2560]{2,1,0:T(8,128)(2,1)} %get-tuple-element.8, bf16[1,640,2560]{2,1,0:T(8,128)(2,1)S(1)} %copy-done.2, bf16[1,640,2560]{2,1,0:T(8,128)(2,1)S(1)} %copy-done.1), kind=kLoop, calls=%fused_computation | loop fusion | flops 19660800 | bytes 26214400 | tf_op jit(solution)/shard_map/stack | solution.py:43
  217.3 12.5 %psum.22 = f32[]{:T(128)} all-reduce(f32[]{:T(128)} %multiply_reduce_fusion), channel_id=1, replica_groups=mesh['dp'=8,'mp'=4] {'mp'}, use_global_device_ids=true, to_apply=%region_3.4 | all-reduce | flops 1 | bytes 8 | tf_op jit(solution)/shard_map/psum | solution.py:47
  230.5 6.7 %fusion.3 = bf16[640,2560,1]{1,0,2:T(8,128)(2,1)} fusion(f32[640,2560]{1,0:T(8,128)} %all-reduce.2.cloned.1.call-done, bf16[128,2560]{1,0:T(8,128)(2,1)} %all_gather.6, f32[]{:T(128)S(6)} %div.7, bf16[128,2560]{1,0:T(8,128)(2,1)} %param.11, bf16[2560,640]{1,0:T(8,128)(2,1)S(1)} %copy-done), kind=kOutput, calls=%fused_computation.7 | convolution fusion | flops 845496320 | bytes 14417924 | tf_op jit(solution)/shard_map/qti,qtj->qij/dot_general | solution.py:49
  237.1 23.7 %fusion.12 = f32[1,4]{1,0:T(1,128)S(1)} fusion(bf16[4,640,2560]{2,1,0:T(8,128)(2,1)} %pad_maximum_fusion, bf16[640,2560,1]{1,0,2:T(8,128)(2,1)} %fusion.3), kind=kOutput, calls=%fused_computation.24 | convolution fusion | flops 13107200 | bytes 16384016 | tf_op jit(solution)/shard_map/qik,sik->qs/dot_general | solution.py:53
  260.9 8.9 %psum.23 = f32[1,4]{1,0:T(1,128)} all-reduce(f32[1,4]{1,0:T(1,128)S(1)} %fusion.12), channel_id=1, replica_groups=mesh['dp'=8,'mp'=4] {'mp'}, use_global_device_ids=true, to_apply=%region_4.5 | all-reduce | flops 4 | bytes 32 | tf_op jit(solution)/shard_map/psum | solution.py:54
  (1 shorter events, 0.0 us)
Async XLA Ops:
  6.5 15.0 %copy-start = (bf16[2560,640]{1,0:T(8,128)(2,1)S(1)}, bf16[2560,640]{1,0:T(8,128)(2,1)}, u32[]{:S(2)}) copy-start(bf16[2560,640]{1,0:T(8,128)(2,1)} %param.13) | copy-start | bytes 9830404
  6.5 6.0 %copy-start.5 = (s32[4]{0:T(128)S(1)}, s32[4]{0:T(128)}, u32[]{:S(2)}) copy-start(s32[4]{0:T(128)} %param.9) | copy-start | bytes 52
  6.5 63.4 %all-gather.2.cloned.1.call-start = ((), (), s32[]{:S(2)}) async-start(), calls=%async_computation | async-start | bytes 3276800 | tf_op jit(solution)/shard_map/all_gather | solution.py:22
  12.5 190.8 %all-reduce.2.cloned.1.call-start = ((), (), s32[]{:S(2)}) async-start(), calls=%async_computation.1 | async-start | bytes 13107200 | tf_op jit(solution)/shard_map/psum | solution.py:46
  69.9 2.8 copy-start.3
  69.9 2.8 copy-start.4
  203.3 5.3 %copy-start.1 = (bf16[1,640,2560]{2,1,0:T(8,128)(2,1)S(1)}, bf16[1,640,2560]{2,1,0:T(8,128)(2,1)}, u32[]{:S(2)}) copy-start(bf16[1,640,2560]{2,1,0:T(8,128)(2,1)} %get-tuple-element.6) | copy-start | bytes 9830404
  203.3 5.3 %copy-start.2 = (bf16[1,640,2560]{2,1,0:T(8,128)(2,1)S(1)}, bf16[1,640,2560]{2,1,0:T(8,128)(2,1)}, u32[]{:S(2)}) copy-start(bf16[1,640,2560]{2,1,0:T(8,128)(2,1)} %get-tuple-element.7) | copy-start | bytes 9830404
Sparse Core Ops, SparseCore 0:
  12.6 57.2 all-gather.1
  97.8 105.4 all-reduce.1
where the time goes:
time: 277 us
  waiting for transfers between devices  129 us (47%)
  matrix products  71.8 us (26%)
  blocking collectives  38.7 us (14%)
  other arithmetic  19.2 us (7%)
  between operations  16.6 us (6%)
    psum x1, waiting for transfers between devices, shards(): curvature = lax.psum(curvature_local, 'dp') * inverse_count  85.4 us
    all_gather x1, waiting for transfers between devices, shards(): lax.all_gather(acts_block, 'mp', axis=1, tiled=True)  43.4 us
    dot_general x4, matrix products, shards(): lax.dot_general(grads_win, acts_win, (((0,), (0,)), ((), ())), preferred_...  27.7 us
    dot_general x1, matrix products, shards(): jnp.einsum('qik,sik->qs', precond, stored, preferred_element_type=jnp.flo...  23.7 us
    all_gather x1, blocking collectives, shards(): lax.all_gather(query_block, 'mp', axis=1, tiled=True)  17.4 us
    dot_general x3, matrix products, rotate(): jnp.dot(values, basis, preferred_element_type=jnp.float32)  13.7 us
    psum x1, blocking collectives, shards(): grand_total = lax.psum(jnp.sum(curvature), 'mp')  12.5 us
    psum x1, blocking collectives, shards(): return lax.psum(partial_value, 'mp')  8.86 us
  transfers between devices with their start and end apart: 2, of which 2 were waited for; matrix products, arithmetic and copies ran while one was open for 5% of the time, Pallas kernels for 0%

commit v1 on v0

--- a/solution.py
+++ b/solution.py
@@ -1,3 +1,4 @@
+import functools
 import jax
 import jax.numpy as jnp
 from jax import lax
@@ -6,6 +7,14 @@
 QUERIES = 1
 QLEN = 128
 damping_ratio = 0.1
+
+
+def update_the_shifts_all(my_tile, a_name):
+    seen_now = lax.all_gather(my_tile, axis_name=a_name)
+    return jnp.sum(seen_now, 0)
+
+
+try_all_the_sites = functools.partial(update_the_shifts_all, a_name="dp")
 
 
 def rotate(values, basis):
@@ -43,7 +52,7 @@
     stored = jnp.stack(stored_list)
     inverse_count = 1.0 / (slot_count * lax.axis_size("dp"))
     query_full = query_rot.reshape(QUERIES, QLEN, -1)
-    curvature = lax.psum(curvature_local, "dp") * inverse_count
+    curvature = try_all_the_sites(curvature_local) * inverse_count
     grand_total = lax.psum(jnp.sum(curvature), "mp")
     damping = damping_ratio * grand_total / (curvature.size * lax.axis_size("mp"))
     local_grad = jnp.einsum(

time: 277 us -> 434 us (1.57)
  waiting for transfers between devices: 129 us -> 263 us
  other arithmetic: 19.2 us -> 42.1 us
    all_gather x0 -> x1, waiting for transfers between devices: none -> 219 us  [update_the_shifts_all(): seen_now = lax.all_gather(my_tile, axis_name=a_name)]
    psum x1 -> x0, waiting for transfers between devices: 85.4 us -> none  [shards(): curvature = lax.psum(curvature_local, 'dp') * inverse_count]
    reduce_sum x0 -> x1, other arithmetic: none -> 22.9 us  [update_the_shifts_all(): return jnp.sum(seen_now, 0)]
  transfers between devices with their start and end apart: 2 -> 2, of which waited for: 2 -> 2; matrix products, arithmetic and copies ran while one was open for 5% -> 3% of each run, Pallas kernels for 0% -> 0%
where the time goes in v1:
time: 434 us
  waiting for transfers between devices  263 us (61%)
  matrix products  71.8 us (17%)
  other arithmetic  42.1 us (10%)
  blocking collectives  38.8 us (9%)
  between operations  16.6 us (4%)
    all_gather x1, waiting for transfers between devices, update_the_shifts_all(): seen_now = lax.all_gather(my_tile, axis_name=a_name)  219 us
    all_gather x1, waiting for transfers between devices, shards(): lax.all_gather(acts_block, 'mp', axis=1, tiled=True)  43.4 us
    dot_general x4, matrix products, shards(): lax.dot_general(grads_win, acts_win, (((0,), (0,)), ((), ())), preferred_...  27.8 us
    dot_general x1, matrix products, shards(): jnp.einsum('qik,sik->qs', precond, stored, preferred_element_type=jnp.flo...  23.7 us
    reduce_sum x1, other arithmetic, update_the_shifts_all(): return jnp.sum(seen_now, 0)  22.9 us
    all_gather x1, blocking collectives, shards(): lax.all_gather(query_block, 'mp', axis=1, tiled=True)  17.4 us
    dot_general x3, matrix products, rotate(): jnp.dot(values, basis, preferred_element_type=jnp.float32)  13.7 us
    psum x1, blocking collectives, shards(): grand_total = lax.psum(jnp.sum(curvature), 'mp')  12.5 us
  transfers between devices with their start and end apart: 2, of which 2 were waited for; matrix products, arithmetic and copies ran while one was open for 3% of the time, Pallas kernels for 0%

profile of v1, /device:TPU:0, one launch (start us, length us, event | category | flops | bytes accessed | tf_op | source)
XLA Modules:
  0.0 433.6 jit_solution(18284254138904770987)
XLA Ops:
  6.5 0.0 copy-start
  6.5 0.0 copy-start.5
  6.5 0.0 all-gather.4.cloned.1.call-start
  6.5 5.9 %convolution_convert_fusion = bf16[512,640]{1,0:T(8,128)(2,1)} fusion(bf16[512,2560]{1,0:T(8,128)(2,1)} %param.7, bf16[2560,640]{1,0:T(8,128)(2,1)} %param.12), kind=kOutput, calls=%fused_computation.12 | convolution fusion | flops 1678049280 | bytes 6553600 | tf_op jit(solution)/shard_map/dot_general | solution.py:21
  12.4 0.0 all-gather.4.cloned.1.call-update
  12.5 0.0 all-gather.6.cloned.1.call-start
  12.5 0.0 copy-done.5
  12.5 0.2 reduce-window.4
  12.7 0.6 fusion.42
  15.9 0.6 fusion.41
  16.5 1.2 compare_and_fusion
  17.7 1.3 compare_and_fusion.1
  19.0 1.3 compare_and_fusion.2
  20.2 1.3 compare_and_fusion.3
  21.5 0.0 copy-done
  21.5 5.0 %convolution_convert_fusion.1 = bf16[512,640]{1,0:T(8,128)(2,1)} fusion(bf16[512,2560]{1,0:T(8,128)(2,1)} %param.8, bf16[2560,640]{1,0:T(8,128)(2,1)S(1)} %copy-done), kind=kOutput, calls=%fused_computation.13 | convolution fusion | flops 1678049280 | bytes 6553600 | tf_op jit(solution)/shard_map/dot_general | solution.py:21
  26.5 43.4 %all-gather.4.cloned.1.call-done = bf16[512,2560]{1,0:T(8,128)(2,1)} async-done(((bf16[512,640]{1,0:T(8,128)(2,1)}), bf16[512,2560]{1,0:T(8,128)(2,1)}) %all-gather.4.cloned.1.call-update) | async-done | bytes 2621456 | tf_op jit(solution)/shard_map/all_gather | solution.py:31
  69.9 0.0 copy-start.3
  69.9 0.0 copy-start.4
  69.9 2.7 fusion.4
  72.7 0.0 copy-done.3
  72.7 0.0 copy-done.4
  72.7 3.9 fusion.6
  76.5 3.9 fusion.8
  80.4 17.3 %multiply_add_fusion = (f32[640,2560]{1,0:T(8,128)}, bf16[1,640,2560]{2,1,0:T(8,128)(2,1)}, bf16[1,640,2560]{2,1,0:T(8,128)(2,1)}, bf16[1,640,2560]{2,1,0:T(8,128)(2,1)}, bf16[1,640,2560]{2,1,0:T(8,128)(2,1)}) fusion(f32[640,2560]{1,0:T(8,128)S(1)} %fusion.4, f32[640,2560]{1,0:T(8,128)} %fusion.6, f32[640,2560]{1,0:T(8,128)} %fusion.8, ...), kind=kOutput, calls=%fused_computation.4 | convolution fusion | flops 857047040 | bytes 40961536 | tf_op jit(solution)/shard_map/dot_general | solution.py:47
  97.7 0.0 all-gather.6.cloned.1.call-update
  97.7 2.8 convolution_convert_fusion.2
  100.6 17.4 %all_gather.12 = bf16[128,2560]{1,0:T(8,128)(2,1)} all-gather(bf16[128,640]{1,0:T(8,128)(2,1)S(1)} %convolution_convert_fusion.2), channel_id=1, replica_groups=mesh['dp'=8,'mp'=4] {'mp'}, dimensions={1}, use_global_device_ids=true | all-gather | bytes 819200 | tf_op jit(solution)/shard_map/all_gather | solution.py:32
  118.0 219.5 %all-gather.6.cloned.1.call-done = f32[5120,2560]{1,0:T(8,128)} async-done(((f32[640,2560]{1,0:T(8,128)}), f32[5120,2560]{1,0:T(8,128)}) %all-gather.6.cloned.1.call-update) | async-done | bytes 52428816 | tf_op jit(solution)/shard_map/all_gather | solution.py:13
  337.4 22.9 %reduce_sum.18 = f32[640,2560]{1,0:T(8,128)} reduce(f32[8,640,2560]{2,1,0:T(8,128)} %bitcast.35, f32[]{:T(128)} %constant.6.clone.1), dimensions={0}, to_apply=%region_1.2 | reduce | flops 11468800 | bytes 58982404 | tf_op jit(solution)/shard_map/reduce_sum | solution.py:14
  360.3 0.0 copy-start.1
  360.4 0.0 copy-start.2
  360.4 5.3 %multiply_reduce_fusion = f32[]{:T(128)} fusion(f32[640,2560]{1,0:T(8,128)} %reduce_sum.18), kind=kLoop, calls=%fused_computation.6 | loop fusion | flops 3276799 | bytes 6553604 | tf_op jit(solution)/shard_map/reduce_sum | solution.py:56
  365.7 0.0 copy-done.1
  365.7 0.0 copy-done.2
  365.7 8.7 %pad_maximum_fusion = bf16[4,640,2560]{2,1,0:T(8,128)(2,1)} fusion(bf16[1,640,2560]{2,1,0:T(8,128)(2,1)} %get-tuple-element.9, bf16[1,640,2560]{2,1,0:T(8,128)(2,1)} %get-tuple-element.8, bf16[1,640,2560]{2,1,0:T(8,128)(2,1)S(1)} %copy-done.2, bf16[1,640,2560]{2,1,0:T(8,128)(2,1)S(1)} %copy-done.1), kind=kLoop, calls=%fused_computation | loop fusion | flops 19660800 | bytes 26214400 | tf_op jit(solution)/shard_map/stack | solution.py:52
  374.4 12.5 %psum.14 = f32[]{:T(128)} all-reduce(f32[]{:T(128)} %multiply_reduce_fusion), channel_id=1, replica_groups=mesh['dp'=8,'mp'=4] {'mp'}, use_global_device_ids=true, to_apply=%region_3.4 | all-reduce | flops 1 | bytes 8 | tf_op jit(solution)/shard_map/psum | solution.py:56
  387.5 6.6 %fusion.3 = bf16[640,2560,1]{1,0,2:T(8,128)(2,1)} fusion(f32[640,2560]{1,0:T(8,128)} %reduce_sum.18, bf16[128,2560]{1,0:T(8,128)(2,1)} %all_gather.12, f32[]{:T(128)S(6)} %div.7, bf16[128,2560]{1,0:T(8,128)(2,1)} %param.11, bf16[2560,640]{1,0:T(8,128)(2,1)S(1)} %copy-done), kind=kOutput, calls=%fused_computation.7 | convolution fusion | flops 845496320 | bytes 14417924 | tf_op jit(solution)/shard_map/qti,qtj->qij/dot_general | solution.py:58
  394.1 23.7 %fusion.12 = f32[1,4]{1,0:T(1,128)S(1)} fusion(bf16[4,640,2560]{2,1,0:T(8,128)(2,1)} %pad_maximum_fusion, bf16[640,2560,1]{1,0,2:T(8,128)(2,1)} %fusion.3), kind=kOutput, calls=%fused_computation.24 | convolution fusion | flops 13107200 | bytes 16384016 | tf_op jit(solution)/shard_map/qik,sik->qs/dot_general | solution.py:62
  417.9 8.9 %psum.15 = f32[1,4]{1,0:T(1,128)} all-reduce(f32[1,4]{1,0:T(1,128)S(1)} %fusion.12), channel_id=1, replica_groups=mesh['dp'=8,'mp'=4] {'mp'}, use_global_device_ids=true, to_apply=%region_4.5 | all-reduce | flops 4 | bytes 32 | tf_op jit(solution)/shard_map/psum | solution.py:63
  (1 shorter events, 0.0 us)
Async XLA Ops:
  6.5 15.0 %copy-start = (bf16[2560,640]{1,0:T(8,128)(2,1)S(1)}, bf16[2560,640]{1,0:T(8,128)(2,1)}, u32[]{:S(2)}) copy-start(bf16[2560,640]{1,0:T(8,128)(2,1)} %param.13) | copy-start | bytes 9830404
  6.5 6.0 %copy-start.5 = (s32[4]{0:T(128)S(1)}, s32[4]{0:T(128)}, u32[]{:S(2)}) copy-start(s32[4]{0:T(128)} %param.9) | copy-start | bytes 52
  6.5 63.4 %all-gather.4.cloned.1.call-start = ((), (), s32[]{:S(2)}) async-start(), calls=%async_computation | async-start | bytes 3276800 | tf_op jit(solution)/shard_map/all_gather | solution.py:31
  12.5 325.0 %all-gather.6.cloned.1.call-start = ((), (), s32[]{:S(2)}) async-start(), calls=%async_computation.1 | async-start | bytes 58982400 | tf_op jit(solution)/shard_map/all_gather | solution.py:13
  69.9 2.7 copy-start.3
  69.9 2.7 copy-start.4
  360.3 5.3 %copy-start.1 = (bf16[1,640,2560]{2,1,0:T(8,128)(2,1)S(1)}, bf16[1,640,2560]{2,1,0:T(8,128)(2,1)}, u32[]{:S(2)}) copy-start(bf16[1,640,2560]{2,1,0:T(8,128)(2,1)} %get-tuple-element.6) | copy-start | bytes 9830404
  360.4 5.3 %copy-start.2 = (bf16[1,640,2560]{2,1,0:T(8,128)(2,1)S(1)}, bf16[1,640,2560]{2,1,0:T(8,128)(2,1)}, u32[]{:S(2)}) copy-start(bf16[1,640,2560]{2,1,0:T(8,128)(2,1)} %get-tuple-element.7) | copy-start | bytes 9830404
Sparse Core Ops, SparseCore 0:
  12.6 57.2 all-gather.3
  97.9 239.5 all-gather.5
